TPU v7x, 32 devices: a whole 2x2x4 slice. The times are simulated.
32 devices in a mesh: data: 2 (over x), seq: 4 (over z), branch: 4 (over y, core).
Axes of the slice: x: 2, y: 2, z: 4, core: 2. Of those that a mesh axis runs over, the one named last changes fastest.
Arguments:
- latents: bfloat16 [2, 1024, 2432], P('data', ('seq', 'branch')), parts along dimension 0
- hint_emb: bfloat16 [2, 1024, 2432], P('data', ('seq', 'branch')), parts along dimension 0
- in_qkv: bfloat16 [2, 3, 2432, 7296], replicated
- in_proj: bfloat16 [2, 3, 38, 64, 2432], replicated
- in_up: bfloat16 [2, 3, 2432, 9728], replicated
- in_down: bfloat16 [2, 3, 9728, 2432], replicated
- out_qkv: bfloat16 [2, 2432, 7296], replicated
- out_proj: bfloat16 [2, 38, 64, 2432], replicated
- out_up: bfloat16 [2, 2432, 9728], replicated
- out_down: bfloat16 [2, 9728, 2432], replicated
- hint_proj: bfloat16 [2432, 2432], replicated
- zero_proj: bfloat16 [3, 2432, 2432], replicated
- skip_proj: bfloat16 [2, 4864, 2432], replicated
- final_proj: bfloat16 [2432, 2432], replicated
Outputs:
- output: bfloat16 [2, 1024, 2432], P('data', ('seq', 'branch')), parts along dimension 0
There are 2 independent parts. A program takes and returns all parts, laid end to end along the dimension named above; an argument that names none is the same for every part.
All inputs are finite; a program needn't handle non-finite values.
Results may differ from a plain program's by a relative error of at most 0.02.
Values are sent between devices in bfloat16 or wider.
A program may use at most 4.75 GiB of HBM per device.

v0:
```python
import functools
import jax
import jax.numpy as jnp
from jax import lax
from jax.experimental import pallas as pl
from jax.experimental.pallas import tpu as pltpu
from jax.sharding import PartitionSpec as P

EPS = 1e-6
D = 2432
HALF_UP = 4864
LANES = 128
TOK = 1024
UNITS = 51
QUERIES = 256
KEYS = 512
MESH_ID = pl.DeviceIdType.MESH
BF16 = jnp.bfloat16
F32 = jnp.float32


def aligned(value, unit):
    return value if isinstance(value, int) else pl.multiple_of(value, unit)


class Chunk:
    def __init__(self, name, parts, room=0):
        self.name, self.parts, self.room = name, parts, room
        self.width = sum(width for width, _ in parts)
        self.blk = self.pos = self.sem = self.trigger = None


class WeightStream:
    def __init__(self, pre, block, post, num_blocks, buf, sem, blank):
        self.buf, self.sem, self.blank, self.num_blocks = buf, sem, blank, num_blocks
        order = []
        sems = {}

        def add(chunks, blk, kind):
            for chunk in chunks:
                item = Chunk(chunk.name, chunk.parts, chunk.room)
                item.blk, item.kind = blk, kind
                item.sem = sems.setdefault(item.name, len(sems))
                order.append(item)

        add(pre, None, 'pre')
        for blk in range(num_blocks):
            add(block, blk, 'block')
        add(post, None, 'post')
        pos = UNITS - sum(chunk.width for chunk in pre)
        holder = [None] * UNITS
        self.first = []
        self.after = {}
        self.places = {}
        for rank, item in enumerate(order):
            if pos + max(item.width, item.room) > UNITS:
                pos = 0
            item.pos, item.rank = pos, rank
            held = [holder[i] for i in range(pos, pos + item.width) if holder[i] is not None]
            holder[pos:pos + item.width] = [item] * item.width
            pos += item.width
            assert self.places.setdefault(item.name, (item.pos, item.width, item.sem)) == (item.pos, item.width, item.sem)
            if not held:
                self.first.append(item)
                continue
            last = max(held, key=lambda other: other.rank)
            self.after.setdefault(last.name, []).append((last.blk, item))
        self.num_sems = len(sems)

    def issue(self, item, blk):
        off = item.pos
        for width, source in item.parts:
            dst = self.buf.at[:, off * LANES:(off + width) * LANES]
            pltpu.make_async_copy(source(blk), dst, self.sem.at[item.sem]).start()
            off += width

    def fill(self, kind):
        for item in self.first:
            if item.kind == kind:
                self.issue(item, item.blk)

    def wait(self, name, trip, width):
        first, _, sem = self.places[(name, 0 if not isinstance(trip, int) else trip)]
        pos = first if isinstance(trip, int) else first + trip * width
        sem = sem if isinstance(trip, int) else sem + trip
        dst = self.buf.at[:, pl.ds(aligned(pos * LANES, LANES), width * LANES)]
        pltpu.make_async_copy(self.blank(width), dst, self.sem.at[sem]).wait()
        return pos

    def row(self, name, trips):
        places = [self.places[(name, trip)] for trip in range(trips)]
        first, width, sem = places[0]
        assert places == [(first + trip * width, width, sem + trip) for trip in range(trips)]

    def used_trip(self, name, trip, trips, blk):
        if isinstance(trip, int):
            self.used((name, trip), blk)
            return
        for k in range(trips):
            if self.after.get((name, k)):
                pl.when(trip == k)(functools.partial(self.used, (name, k), blk))

    def used(self, name, blk):
        todo = self.after.get(name, [])
        if blk is None or isinstance(blk, int):
            for last_blk, item in todo:
                if last_blk == blk:
                    self.issue(item, item.blk)
            return
        seen = set()
        for last_blk, item in todo:
            if item.kind == 'post':
                assert last_blk == self.num_blocks - 1
                pl.when(blk == last_blk)(lambda item=item: self.issue(item, None))
                continue
            step = item.blk - last_blk
            if (item.name, step) in seen:
                continue
            seen.add((item.name, step))
            if step == 0:
                self.issue(item, blk)
            else:
                pl.when(blk < self.num_blocks - 1)(lambda item=item: self.issue(item, blk + 1))


def matmul(lhs, rhs):
    return jnp.dot(lhs, rhs, preferred_element_type=F32)


def add_f32(left, right):
    return left.astype(F32) + right.astype(F32)


def ln_rows(src, dst, first, rows):
    for r0 in range(0, rows, 32):
        at = pl.ds(aligned(first + r0, 32), 32)
        val = src[at, :].astype(F32)
        cen = val - jnp.mean(val, axis=-1, keepdims=True)
        var = jnp.mean(cen * cen, axis=-1, keepdims=True)
        dst[at, :] = (cen * lax.rsqrt(var + EPS)).astype(BF16)


def step_kernel(num_in, lat, hint, in_qkv, in_proj, in_up, in_down, out_qkv, out_proj, out_up, out_down, hint_w, zero_w, skip_w, final_w, y_ref,
                wbuf, xl, hi, msg, u, x, act, po, ps, pin, qin, stg, o_st, a_in, vt, sb, part, rx, skp,
                wsem, init_sem, xs_sem, xr_sem, us_sem, ur_sem, qs_sem, qr_sem, as_sem, ar_sem, ps_sem, pr_sem, es_sem, er_sem):
    data_id = lax.axis_index('data')
    seq_id = lax.axis_index('seq')
    branch_id = lax.axis_index('branch')
    core = branch_id % 2
    row_y = branch_id // 2
    side = seq_id // 2
    quad = 2 * row_y + seq_id % 2
    chip = 4 * side + quad

    def device(side_id, quad_id, core_id):
        return (data_id, 2 * side_id + quad_id % 2, 2 * (quad_id // 2) + core_id)

    peer = device(side, quad, 1 - core)
    partner = device(1 - side, quad, core)

    def remote(src, dst, send, recv, dev):
        return pltpu.make_async_remote_copy(src_ref=src, dst_ref=dst, send_sem=send, recv_sem=recv, device_id=dev, device_id_type=MESH_ID)

    def layout(is_in):
        n_chips = 4 if is_in else 8
        me = quad if is_in else chip
        bits = 2 if is_in else 3

        def extra_dest(idx):
            return 2 * idx + core if is_in else 1 + 5 * idx + 3 * core

        def combo(j):
            trip, odd = j // 2, j % 2
            extra = trip // 4
            half = n_chips // 2
            rel = (half - 1) - trip % half
            top = me // 2
            prim = (top + rel) % 2 if is_in else 2 * ((top // 2 + rel // 2) % 2) + (top + rel) % 2
            prim = 2 * prim + odd
            slot_p = trip // half
            idx = odd - core
            dest = (1 - extra) * prim + extra * extra_dest(idx)
            slot = (1 - extra) * slot_p + extra * (8 // n_chips)
            num = (1 - extra) * (10 * core + slot_p * n_chips + prim) + extra * (10 * core + 8 + idx)
            return dest, slot, num, extra * core * (1 - odd) == 0

        def owner(num):
            plane, j = num // 10, num % 10
            extra = j // 8
            left = 2 * (j - 8) + plane if is_in else 1 + 5 * (j - 8) + 3 * plane
            return plane, (1 - extra) * (j % n_chips) + extra * left

        return n_chips, me, combo, owner, extra_dest

    def chip_device(is_in, idx, core_id):
        return device(side, idx, core_id) if is_in else device(idx // 4, idx % 4, core_id)

    num_blocks = num_in + 1
    num_out = num_in

    def cols(start):
        return pl.ds(aligned(start, LANES), LANES)

    def wide(start, width):
        return pl.ds(aligned(start, LANES), width * LANES)

    WIDE = (8, 8, 3)
    NARROW = (4, 4, 4, 4, 3)

    def square(name, source, widths=WIDE):
        out, first = [], 0
        for trip, width in enumerate(widths):
            out.append(Chunk((name, trip), [(width, lambda blk, first=first, width=width: source(blk, wide(first * LANES, width)))], 16 if trip == 0 else 0))
            first += width
        return out

    def qkv_chunks(name, combo, source):
        out = []
        for trip in range(5):
            num = combo(2 * trip)[2]
            out.append(Chunk((name, trip), [(2, lambda blk, num=num, part=part: source(blk, wide(part * D + num * LANES, 2))) for part in range(3)], 30 if trip == 0 else 0))
        return out

    UP_TRIPS = (8, 8, 8, 8, 6)
    DOWN_TRIPS = (4, 4, 4, 4, 3)

    def up_chunks(name, source):
        out, first = [], 0
        for trip, width in enumerate(UP_TRIPS):
            out.append(Chunk((name, trip), [(width, lambda blk, first=first, width=width: source(blk, wide(core * HALF_UP + first * LANES, width)))], 32 if trip == 0 else 0))
            first += width
        return out

    def down_chunks(name, source):
        out, first = [], 0
        for trip, width in enumerate(DOWN_TRIPS):
            out.append(Chunk((name, trip), [
                (width, lambda blk, first=first, width=width, k=k: source(blk, pl.ds(aligned(core * HALF_UP + k * D, LANES), D), wide(first * LANES, width)))
                for k in range(2)], 32 if trip == 0 else 0))
            first += width
        return out

    in_combo, out_combo = layout(True)[2], layout(False)[2]
    pre = square('hint', lambda blk, c: hint_w.at[:, c])
    block = (qkv_chunks('in_qkv', in_combo, lambda blk, c: in_qkv.at[side, blk, :, c])
             + square('in_zero', lambda blk, c: zero_w.at[(blk + num_in) % num_blocks, :, c], NARROW)
             + square('in_proj', lambda blk, c: in_proj.at[side, blk, :, c])
             + up_chunks('in_up', lambda blk, c: in_up.at[side, blk, :, c])
             + down_chunks('in_down', lambda blk, r, c: in_down.at[side, blk, r, c]))

    def skip_square(idx, half):
        return square(('skip', idx, half), lambda blk, c: skip_w.at[idx, pl.ds(half * D, D), c], NARROW if half else WIDE)

    post = square('zero', lambda blk, c: zero_w.at[num_in, :, c]) + skip_square(0, 1) + skip_square(0, 0)
    for idx in range(num_out):
        post += qkv_chunks(('qkv', idx), out_combo, lambda blk, c, idx=idx: out_qkv.at[idx, :, c])
        if idx + 1 < num_out:
            post += skip_square(idx + 1, 1)
        post += square(('proj', idx), lambda blk, c, idx=idx: out_proj.at[idx, :, c])
        post += up_chunks(('up', idx), lambda blk, c, idx=idx: out_up.at[idx, :, c])
        post += down_chunks(('down', idx), lambda blk, r, c, idx=idx: out_down.at[idx, r, c])
        if idx + 1 < num_out:
            post += skip_square(idx + 1, 0)
    post += square('final', lambda blk, c: final_w.at[:, c])
    stream = WeightStream(pre, block, post, num_blocks, wbuf, wsem, lambda width: in_up.at[0, 0, :, 0:width * LANES])

    def columns(pos, width):
        return wbuf[:, pl.ds(aligned(pos * LANES, LANES), width * LANES)]

    def mm(blk, name, looped, widths, lhs, emit, done=None, k_subs=1):
        stream.row(name, looped)

        def trip(t, col, width):
            pos = stream.wait(name, t, width * k_subs)
            for first in range(0, width, 2):
                size = min(2, width - first)
                subs = [columns(pos + k * width + first, size) for k in range(k_subs)]
                rhs = subs[0] if k_subs == 1 else jnp.concatenate(subs, axis=0)
                emit(aligned(col + first * LANES, LANES), size * LANES, matmul(lhs(), rhs))
            if done is not None:
                done(aligned(col, LANES), width * LANES)
            stream.used_trip(name, t, looped, blk)

        pl.loop(0, looped)(lambda t: trip(t, t * (widths[0] * LANES), widths[0]))
        col = looped * widths[0] * LANES
        for t in range(looped, len(widths)):
            trip(t, col, widths[t])
            col += widths[t] * LANES

    def mm_square(blk, name, lhs, emit, done=None, widths=WIDE):
        mm(blk, name, len(widths) - 1, widths, lhs, emit, done)

    def mm_up(blk, name, lhs, emit):
        mm(blk, name, 4, UP_TRIPS, lhs, emit)

    def mm_down(blk, name, lhs, emit, done):
        mm(blk, name, 4, DOWN_TRIPS, lhs, emit, done, 2)

    def each(widths, fn):
        col = 0
        for width in widths:
            fn(col, width * LANES)
            col += width * LANES

    scope = jax.named_scope
    get_lat = pltpu.make_async_copy(lat.at[0], xl, init_sem.at[0])
    get_hint = pltpu.make_async_copy(hint.at[0], hi, init_sem.at[1])
    with scope('barrier'):
        get_hint.start()
        get_lat.start()
        stream.fill('pre')
        barrier = pltpu.get_barrier_semaphore()
        my_index = seq_id * 4 + branch_id
        for k in range(1, 16):
            other = (my_index + k) % 16
            pl.semaphore_signal(barrier, inc=1, device_id=(data_id, other // 4, other % 4), device_id_type=MESH_ID)
        pl.semaphore_wait(barrier, 15)
        get_lat.wait()
        get_hint.wait()

    mine = pl.ds(pl.multiple_of(side * 64, 64), 64)
    theirs = pl.ds(pl.multiple_of((1 - side) * 64, 64), 64)

    def swap_copy(col, width):
        return remote(msg.at[:, pl.ds(col, width)], u.at[mine, pl.ds(col, width)], us_sem.at[col // 1024], ur_sem.at[col // 1024], partner)

    def emit_hint(col, width, acc):
        base_in = xl[:, pl.ds(col, width)]
        control_in = add_f32(base_in, acc.astype(BF16)).astype(BF16)
        is_base = side == 0
        u[mine, pl.ds(col, width)] = jnp.where(is_base, base_in, control_in)
        msg[:, pl.ds(col, width)] = jnp.where(is_base, control_in, base_in)

    with scope('hint'):
        mm_square(None, 'hint', lambda: hi[...], emit_hint, lambda col, width: swap_copy(col, width).start())
        stream.fill('block')
    def exchange_half(half, first, size, rows):
        ln_rows(u, x, first, size)
        send = remote(x.at[pl.ds(first, size)], x.at[pl.ds(aligned(first + rows, 32), size)], xs_sem.at[half], xr_sem.at[half], peer)
        send.start()
        return send

    def exchange_rows(rows):
        sends = [exchange_half(half, half * (rows // 2), rows // 2, rows) for half in range(2)]
        for send in sends:
            send.wait_recv()
        return sends

    def run_block(is_in, blk, names, bank, fill_in, before_proj):
        rows = 128 if is_in else 64
        chip_rows = 2 * rows
        n_chips, me, combo, owner, extra_dest = layout(is_in)
        extra_slot = 8 // n_chips
        qkv_name, proj_name, up_name, down_name = names

        def chunk(idx, size):
            return pl.ds(aligned(idx * size, size), size)

        def piece_copy(j, dest, slot):
            at = 3 * bank + slot
            return remote(stg.at[j, pl.ds(0, chip_rows)], qin.at[at, chunk(me, chip_rows)], qs_sem.at[j], qr_sem.at[at, me], chip_device(is_in, dest, core))

        def qkv_trip(trip):
            pos = stream.wait(qkv_name, trip, 6)
            for part in range(3):
                both = matmul(x[0:chip_rows, :], columns(pos + 2 * part, 2)).astype(BF16)
                stg[2 * trip, 0:chip_rows, part * LANES:(part + 1) * LANES] = both[:, 0:LANES]
                stg[2 * trip + 1, 0:chip_rows, part * LANES:(part + 1) * LANES] = both[:, LANES:2 * LANES]
            for j in (2 * trip, 2 * trip + 1):
                dest, slot, num, valid = combo(j)

                @pl.when(jnp.logical_and(valid, dest != me))
                def _(j=j, dest=dest, slot=slot):
                    piece_copy(j, dest, slot).start()

                @pl.when(jnp.logical_and(valid, dest == me))
                def _(j=j, slot=slot):
                    qin[3 * bank + slot, chunk(me, chip_rows), :] = stg[j, 0:chip_rows, :]

            stream.used_trip(qkv_name, trip, 5, blk)

        def norm_and_qkv():
            with scope('ln1'):
                sends = exchange_rows(rows)
            with scope('qkv'):
                stream.row(qkv_name, 5)
                pl.loop(0, 5)(qkv_trip)
            for send in sends:
                send.wait_send()

        if is_in:
            pl.when(blk > 0)(norm_and_qkv)
        else:
            norm_and_qkv()
        with scope('fill'):
            fill_in()

        holds = [(extra_dest(0) == me).astype(jnp.int32), jnp.logical_and(extra_dest(1) == me, core == 0).astype(jnp.int32)]
        num_slots = extra_slot + holds[0] + holds[1]

        def slot_pair(slot):
            extra = slot // extra_slot
            return (1 - extra) * (10 * core + slot * n_chips + me) + extra * (10 * core + 8 + holds[1])

        per_chunk = QUERIES // chip_rows

        def query_chunk(i):
            return (me // per_chunk + 1 + i) % (TOK // QUERIES)

        def send_copies(slot, i):
            copies = []
            num = slot_pair(slot)
            first = query_chunk(i) * per_chunk
            chips = [(first + n, True) for n in range(per_chunk)]
            if i == TOK // QUERIES - 1:
                chips = [(me, False)] if per_chunk == 1 else [(me + 1 - 2 * (me % 2), True), (me, False)]
            for n, (idx, other) in enumerate(chips):
                for which in range(2):
                    if not other and which == 0:
                        continue
                    to_core = core if which == 0 else 1 - core
                    src = o_st.at[slot, pl.ds(pl.multiple_of(idx * chip_rows + which * rows, rows), rows)]
                    copies.append(remote(src, a_in.at[pl.ds(0, rows), cols(num * LANES)], as_sem.at[slot, 4 * i + 2 * n + which], ar_sem.at[num], chip_device(is_in, idx, to_core)))
            return copies

        def attend(slot):
            at = 3 * bank + slot
            with scope('att_wait'):
                for k in range(1, n_chips):
                    src = (me + k) % n_chips
                    remote(stg.at[0, pl.ds(0, chip_rows)], qin.at[at, chunk(src, chip_rows)], qs_sem.at[0], qr_sem.at[at, src], peer).wait_recv()
            vt[...] = qin[at, :, 2 * LANES:3 * LANES].T
            low = lax.broadcasted_iota(jnp.int32, (QUERIES, LANES), 1) < 64

            def trip(now, after, top):
                top_next = total = out_a = out_b = None
                if after is not None:
                    q_pair = (qin[at, chunk(query_chunk(after), QUERIES), 0:LANES].astype(F32) * 0.125).astype(BF16)
                    none = jnp.zeros_like(q_pair)
                    q_both = jnp.concatenate([jnp.where(low, q_pair, none), jnp.where(low, none, q_pair)], axis=0)
                for k0 in range(0, TOK, KEYS):
                    keys = slice(k0, k0 + KEYS)
                    if after is not None:
                        score = lax.dot_general(qin[at, keys, LANES:2 * LANES], q_both, (((1,), (1,)), ((), ())), preferred_element_type=F32)
                        sb[after % 2, keys, :] = score
                        part_top = jnp.max(score.reshape(KEYS // 8, 8, 2 * QUERIES), axis=0)
                        top_next = part_top if top_next is None else jnp.maximum(top_next, part_top)
                    if now is not None:
                        weight = jnp.exp(sb[now % 2, keys, :] - top)
                        part_sum = jnp.sum(weight.reshape(KEYS // 8, 8, 2 * QUERIES), axis=0)
                        total = part_sum if total is None else total + part_sum
                        prob = weight.astype(BF16)
                        term_a = matmul(vt[0:64, keys], prob[:, 0:QUERIES])
                        term_b = matmul(vt[64:128, keys], prob[:, QUERIES:2 * QUERIES])
                        out_a = term_a if out_a is None else out_a + term_a
                        out_b = term_b if out_b is None else out_b + term_b
                if now is not None:
                    inv = 1.0 / jnp.sum(total, axis=0, keepdims=True)
                    mixed = jnp.concatenate([out_a * inv[:, 0:QUERIES], out_b * inv[:, QUERIES:2 * QUERIES]], axis=0)
                    o_st[slot, chunk(query_chunk(now), QUERIES), :] = mixed.T.astype(BF16)
                    for copy in send_copies(slot, now):
                        copy.start()
                return None if after is None else jnp.max(top_next, axis=0, keepdims=True)

            last = TOK // QUERIES - 1
            top = trip(None, 0, None)
            for i in range(last):
                top = trip(i, i + 1, top)
            trip(last, None, top)
            a_in[0:rows, cols(slot_pair(slot) * LANES)] = o_st[slot, pl.ds(pl.multiple_of(me * chip_rows, chip_rows), rows), :]

        with scope('att'):
            pl.loop(0, num_slots)(attend)

        with scope('await'):
            @pl.loop(0, 10)
            def _(j):
                dest, slot, num, valid = combo(j)

                @pl.when(jnp.logical_and(valid, dest != me))
                def _():
                    piece_copy(j, dest, slot).wait_send()

            @pl.loop(0, 19)
            def _(num):
                plane, dest = owner(num)

                @pl.when(jnp.logical_not(jnp.logical_and(core == plane, me == dest)))
                def _():
                    remote(o_st.at[0, pl.ds(0, rows)], a_in.at[pl.ds(0, rows), cols(num * LANES)], as_sem.at[0, 0], ar_sem.at[num], peer).wait_recv()

            before_proj()

        def emit_proj(col, width, acc):
            u[0:rows, pl.ds(col, width)] = add_f32(u[0:rows, pl.ds(col, width)], acc.astype(BF16)).astype(BF16)

        with scope('proj'):
            mm_square(blk, proj_name, lambda: a_in[0:rows, :], emit_proj)

            @pl.loop(0, num_slots)
            def _(slot):
                for i in range(TOK // QUERIES):
                    for copy in send_copies(slot, i):
                        copy.wait_send()

        with scope('ln2'):
            sends = exchange_rows(rows)

        def emit_up(col, width, acc):
            hidden = acc.astype(BF16).astype(F32)
            act[0:chip_rows, pl.ds(col, width)] = jax.nn.gelu(hidden).astype(BF16)

        with scope('up'):
            mm_up(blk, up_name, lambda: x[0:chip_rows, :], emit_up)
            for send in sends:
                send.wait_send()

        def partial_copy(col, width):
            tile = col // 512
            return remote(ps.at[pl.ds(0, rows), pl.ds(col, width)], pin.at[pl.ds(0, rows), pl.ds(col, width)], ps_sem.at[tile], pr_sem.at[tile], peer)

        def emit_down(col, width, acc):
            po[0:rows, pl.ds(col, width)] = acc[0:rows]
            ps[0:rows, pl.ds(col, width)] = acc[rows:chip_rows]

        with scope('down'):
            mm_down(blk, down_name, lambda: act[0:chip_rows, :], emit_down, lambda col, width: partial_copy(col, width).start())

        def finish(col, width):
            partial_copy(col, width).wait()
            total = (po[0:rows, pl.ds(col, width)] + pin[0:rows, pl.ds(col, width)]).astype(BF16)
            u[0:rows, pl.ds(col, width)] = add_f32(u[0:rows, pl.ds(col, width)], total).astype(BF16)

        with scope('fin'):
            pl.loop(0, 4)(lambda t: finish(aligned(t * 512, 512), 512))
            finish(4 * 512, 384)

    def make_part(blk, name, idx, after=None, widths=WIDE):
        def emit(col, width, acc):
            part[idx, :, pl.ds(col, width)] = jnp.where(side == 0, u[:, pl.ds(col, width)], acc.astype(BF16))
        mm_square(blk, name, lambda: u[...], emit, after, widths)

    def part_copy(idx):
        return remote(part.at[idx, theirs], rx.at[idx], es_sem.at[idx], er_sem.at[idx], partner)

    def mid_copy(col, width):
        tile = num_in + col // 1024
        return remote(part.at[num_in, theirs, pl.ds(col, width)], rx.at[num_in, :, pl.ds(col, width)], es_sem.at[tile], er_sem.at[tile], partner)

    nothing = lambda: None

    def first_qkv():
        n_chips, me, combo, _, _ = layout(True)

        def piece_copies(j, dest, slot, off):
            return [remote(stg.at[j, pl.ds(pl.multiple_of(off + at, 64), 64)], qin.at[slot, pl.ds(pl.multiple_of(me * 256 + off + at, 64), 64)],
                           qs_sem.at[j], qr_sem.at[slot, me], device(side, dest, core)) for at in (0, 128)]

        stream.row('in_qkv', 5)
        base = stream.places[('in_qkv', 0)][0]

        @pl.loop(0, 2)
        def _(half):
            off = (side + half) % 2 * 64

            @pl.when(half == 1)
            def _():
                each(WIDE, lambda col, width: swap_copy(col, width).wait())

            send = exchange_half(half, pl.multiple_of(off, 64), 64, 128)
            send.wait_recv()
            own, other = pl.ds(pl.multiple_of(off, 64), 64), pl.ds(pl.multiple_of(128 + off, 64), 64)

            @pl.loop(0, 5)
            def _(t):
                pl.when(half == 0)(lambda: (stream.wait('in_qkv', t, 6), None)[1])
                for part in range(3):
                    lhs = jnp.concatenate([x[own, :], x[other, :]], axis=0)
                    both = matmul(lhs, columns(base + 6 * t + 2 * part, 2)).astype(BF16)
                    for odd in range(2):
                        stg[2 * t + odd, own, part * LANES:(part + 1) * LANES] = both[0:64, odd * LANES:(odd + 1) * LANES]
                        stg[2 * t + odd, other, part * LANES:(part + 1) * LANES] = both[64:128, odd * LANES:(odd + 1) * LANES]
                for j in (2 * t, 2 * t + 1):
                    dest, slot, num, valid = combo(j)

                    @pl.when(jnp.logical_and(valid, dest != me))
                    def _(j=j, dest=dest, slot=slot):
                        for copy in piece_copies(j, dest, slot, off):
                            copy.start()

                    @pl.when(jnp.logical_and(valid, dest == me))
                    def _(j=j, slot=slot):
                        for at in (0, 128):
                            qin[slot, pl.ds(pl.multiple_of(me * 256 + off + at, 64), 64), :] = stg[j, pl.ds(pl.multiple_of(off + at, 64), 64), :]
                pl.when(half == 1)(lambda: stream.used_trip('in_qkv', t, 5, 0))

            send.wait_send()

    first_qkv()

    @pl.loop(0, num_blocks)
    def _(blk):
        def send_part():
            pl.when(blk > 0)(lambda: part_copy(blk - 1).start())

        run_block(True, blk, ('in_qkv', 'in_proj', 'in_up', 'in_down'), blk % 2, lambda: make_part(blk, 'in_zero', (blk + num_in) % num_blocks, widths=NARROW), send_part)

    with scope('midpart'):
        make_part(None, 'zero', num_in, lambda col, width: mid_copy(col, width).start())
        for idx in range(num_in):
            part_copy(idx).wait()
            rx[idx] = add_f32(part[idx, mine, :], rx[idx]).astype(BF16)

    def skip_part(blk):
        def emit(col, width, acc):
            skp[:, pl.ds(col, width)] = acc
        mm_square(None, ('skip', blk, 1), lambda: rx[num_in - 1 - blk], emit, widths=NARROW)

    def merge(blk):
        def emit(col, width, acc):
            msg[:, pl.ds(col, width)] = (skp[:, pl.ds(col, width)] + acc).astype(BF16)
        mm_square(None, ('skip', blk, 0), lambda: u[0:64, :], emit)
        u[0:64, :] = msg[...]

    with scope('skip0'):
        skip_part(0)

    def mid_sum(col, width):
        mid_copy(col, width).wait()
        u[0:64, pl.ds(col, width)] = add_f32(part[num_in, mine, pl.ds(col, width)], rx[num_in, :, pl.ds(col, width)]).astype(BF16)

    with scope('midwait'):
        each(WIDE, mid_sum)
    for blk in range(num_out):
        with scope('merge'):
            merge(blk)
        run_block(False, None, (('qkv', blk), ('proj', blk), ('up', blk), ('down', blk)), (num_blocks + blk) % 2, functools.partial(skip_part, blk + 1) if blk + 1 < num_out else nothing, nothing)

    def emit_final(col, width, acc):
        y_ref[0, :, pl.ds(col, width)] = acc.astype(BF16)

    with scope('final'):
        ln_rows(u, x, 0, 64)
        mm_square(None, 'final', lambda: x[0:64, :], emit_final)


def solution(mesh):
    row_spec = P('data', ('seq', 'branch'), None)

    def device_fn(latents, hint_emb, in_qkv, in_proj, in_up, in_down, out_qkv, out_proj, out_up, out_down, hint_proj, zero_proj, skip_proj, final_proj):
        num_in = out_qkv.shape[0]
        in_proj = in_proj.reshape(2, num_in + 1, D, D)
        out_proj = out_proj.reshape(num_in, D, D)
        anywhere = pl.BlockSpec(memory_space=pl.ANY)
        dma = pltpu.SemaphoreType.DMA
        return pl.pallas_call(
            functools.partial(step_kernel, num_in),
            out_shape=jax.ShapeDtypeStruct((1, 64, D), BF16),
            in_specs=[anywhere] * 14,
            out_specs=pl.BlockSpec(memory_space=pltpu.VMEM),
            scratch_shapes=[
                pltpu.VMEM((D, UNITS * LANES), BF16),
                pltpu.VMEM((64, D), BF16),
                pltpu.VMEM((64, D), BF16),
                pltpu.VMEM((64, D), BF16),
                pltpu.VMEM((128, D), BF16),
                pltpu.VMEM((256, D), BF16),
                pltpu.VMEM((256, HALF_UP), BF16),
                pltpu.VMEM((128, D), F32),
                pltpu.VMEM((128, D), F32),
                pltpu.VMEM((128, D), F32),
                pltpu.VMEM((6, TOK, 3 * LANES), BF16),
                pltpu.VMEM((10, 256, 3 * LANES), BF16),
                pltpu.VMEM((3, TOK, LANES), BF16),
                pltpu.VMEM((128, D), BF16),
                pltpu.VMEM((LANES, TOK), BF16),
                pltpu.VMEM((2, TOK, 2 * QUERIES), F32),
                pltpu.VMEM((num_in + 1, 128, D), BF16),
                pltpu.VMEM((num_in + 1, 64, D), BF16),
                pltpu.VMEM((64, D), F32),
                dma((100,)), dma((2,)), dma((2,)), dma((2,)), dma((10,)), dma((10,)),
                dma((10,)), dma((6, 8)), dma((3, 16)), dma((19,)),
                dma((10,)), dma((10,)), dma((num_in + 10,)), dma((num_in + 10,)),
            ],
            compiler_params=pltpu.CompilerParams(collective_id=0, has_side_effects=True, vmem_limit_bytes=67043328),
            name='denoiser_step',
        )(latents, hint_emb, in_qkv, in_proj, in_up, in_down, out_qkv, out_proj, out_up, out_down, hint_proj, zero_proj, skip_proj, final_proj)

    return jax.shard_map(device_fn, mesh=mesh, in_specs=(row_spec, row_spec) + (P(),) * 12, out_specs=row_spec, check_vma=False)
```

profile of v0, /device:TPU:0, one launch (start us, length us, event | category | flops | bytes accessed | tf_op | source)
XLA Modules:
  0.0 316.7 jit_solution(9793667158606103534)
XLA Ops:
  0.0 315.0 %denoiser_step.1 = bf16[1,64,2432]{2,1,0:T(8,128)(2,1)} custom-call(bf16[1,64,2432]{2,1,0:T(8,128)(2,1)} %lat.1, bf16[1,64,2432]{2,1,0:T(8,128)(2,1)} %hint.1, bf16[2,3,2432,7296]{3,2,1,0:T(8,128)(2,1)} %in_qkv.1, bf16[2,3,2432,2432]{3,2,1,0:T(8,128)(2,1)} %bitcast.in_proj, bf16[2,3,2432,9728]{3,2,1,0:T(8,128)(2,1)} %in_up.1, ...), custom_call_target="tpu_custom_call" | custom-call | tf_op jit(solution)/shard_map/denoiser_step/pallas_call | solution.py:656
  315.0 1.7 copy.16
where the time goes:
time: 317 us
  Pallas kernels  315 us (99%)
    pallas_call x1, Pallas kernels, device_fn(): pl.pallas_call(functools.partial(step_kernel, num_in), out_shape=jax.Shap...  315 us

commit v1 on v0

--- a/solution.py
+++ b/solution.py
@@ -210,7 +210,7 @@
     def square(name, source, widths=WIDE):
         out, first = [], 0
         for trip, width in enumerate(widths):
-            out.append(Chunk((name, trip), [(width, lambda blk, first=first, width=width: source(blk, wide(first * LANES, width)))], 16 if trip == 0 else 0))
+            out.append(Chunk((name, trip), [(width, lambda blk, first=first, width=width: source(blk, wide(first * LANES, width)))], 19 if trip == 0 else 0))
             first += width
         return out
 
@@ -244,7 +244,7 @@
     pre = square('hint', lambda blk, c: hint_w.at[:, c])
     block = (qkv_chunks('in_qkv', in_combo, lambda blk, c: in_qkv.at[side, blk, :, c])
              + square('in_zero', lambda blk, c: zero_w.at[(blk + num_in) % num_blocks, :, c], NARROW)
-             + square('in_proj', lambda blk, c: in_proj.at[side, blk, :, c])
+             + square('in_proj', lambda blk, c: in_proj.at[side, blk, :, c], NARROW)
              + up_chunks('in_up', lambda blk, c: in_up.at[side, blk, :, c])
              + down_chunks('in_down', lambda blk, r, c: in_down.at[side, blk, r, c]))
 
@@ -256,7 +256,7 @@
         post += qkv_chunks(('qkv', idx), out_combo, lambda blk, c, idx=idx: out_qkv.at[idx, :, c])
         if idx + 1 < num_out:
             post += skip_square(idx + 1, 1)
-        post += square(('proj', idx), lambda blk, c, idx=idx: out_proj.at[idx, :, c])
+        post += square(('proj', idx), lambda blk, c, idx=idx: out_proj.at[idx, :, c], NARROW)
         post += up_chunks(('up', idx), lambda blk, c, idx=idx: out_up.at[idx, :, c])
         post += down_chunks(('down', idx), lambda blk, r, c, idx=idx: out_down.at[idx, r, c])
         if idx + 1 < num_out:
@@ -264,22 +264,26 @@
     post += square('final', lambda blk, c: final_w.at[:, c])
     stream = WeightStream(pre, block, post, num_blocks, wbuf, wsem, lambda width: in_up.at[0, 0, :, 0:width * LANES])
 
-    def columns(pos, width):
-        return wbuf[:, pl.ds(aligned(pos * LANES, LANES), width * LANES)]
-
-    def mm(blk, name, looped, widths, lhs, emit, done=None, k_subs=1):
+    def columns(pos, width, pick=None):
+        cut = pl.ds(aligned(pos * LANES, LANES), width * LANES)
+        if pick is None:
+            return wbuf[:, cut]
+        return jnp.concatenate([wbuf[first:last, cut] for first, last in pick], axis=0)
+
+    def mm(blk, name, looped, widths, lhs, emit, done=None, k_subs=1, pick=None):
         stream.row(name, looped)
 
         def trip(t, col, width):
             pos = stream.wait(name, t, width * k_subs)
             for first in range(0, width, 2):
                 size = min(2, width - first)
-                subs = [columns(pos + k * width + first, size) for k in range(k_subs)]
+                subs = [columns(pos + k * width + first, size, pick) for k in range(k_subs)]
                 rhs = subs[0] if k_subs == 1 else jnp.concatenate(subs, axis=0)
                 emit(aligned(col + first * LANES, LANES), size * LANES, matmul(lhs(), rhs))
             if done is not None:
                 done(aligned(col, LANES), width * LANES)
-            stream.used_trip(name, t, looped, blk)
+            if pick is None:
+                stream.used_trip(name, t, looped, blk)
 
         pl.loop(0, looped)(lambda t: trip(t, t * (widths[0] * LANES), widths[0]))
         col = looped * widths[0] * LANES
@@ -481,21 +485,38 @@
                 def _():
                     piece_copy(j, dest, slot).wait_send()
 
-            @pl.loop(0, 19)
-            def _(num):
+            def wait_heads(num):
                 plane, dest = owner(num)
 
                 @pl.when(jnp.logical_not(jnp.logical_and(core == plane, me == dest)))
                 def _():
                     remote(o_st.at[0, pl.ds(0, rows)], a_in.at[pl.ds(0, rows), cols(num * LANES)], as_sem.at[0, 0], ar_sem.at[num], peer).wait_recv()
 
+            pl.loop(0, 16)(lambda n: wait_heads(n + 2 * (n // 8)))
+
+        main, left = ((0, 1024), (1280, 2304)), ((1024, 1280), (2304, 2432))
+
+        def heads(pick):
+            return jnp.concatenate([a_in[0:rows, first:last] for first, last in pick], axis=1)
+
+        def emit_main(col, width, acc):
+            po[0:rows, pl.ds(col, width)] = acc
+
+        with scope('proj_main'):
+            mm(blk, proj_name, 4, NARROW, lambda: heads(main), emit_main, pick=main)
+        with scope('await_left'):
+            for num in (8, 9, 18):
+                wait_heads(num)
             before_proj()
-
-        def emit_proj(col, width, acc):
-            u[0:rows, pl.ds(col, width)] = add_f32(u[0:rows, pl.ds(col, width)], acc.astype(BF16)).astype(BF16)
-
         with scope('proj'):
-            mm_square(blk, proj_name, lambda: a_in[0:rows, :], emit_proj)
+            first_unit = stream.places[(proj_name, 0)][0]
+            for unit in range(0, 19, 2):
+                size = min(2, 19 - unit)
+                cut = slice(unit * LANES, (unit + size) * LANES)
+                acc = po[0:rows, cut] + matmul(heads(left), columns(first_unit + unit, size, left))
+                u[0:rows, cut] = add_f32(u[0:rows, cut], acc.astype(BF16)).astype(BF16)
+            for trip in range(5):
+                stream.used((proj_name, trip), blk)
 
             @pl.loop(0, num_slots)
             def _(slot):

time: 317 us -> 311 us (0.981)
  Pallas kernels: 315 us -> 309 us
    pallas_call x1, Pallas kernels: 315 us -> 309 us  [device_fn(): pl.pallas_call(functools.partial(step_kernel, num_in), out_shape=jax.Shap...]
where the time goes in v1:
time: 311 us
  Pallas kernels  309 us (99%)
    pallas_call x1, Pallas kernels, device_fn(): pl.pallas_call(functools.partial(step_kernel, num_in), out_shape=jax.Shap...  309 us

profile of v1, /device:TPU:0, one launch (start us, length us, event | category | flops | bytes accessed | tf_op | source)
XLA Modules:
  0.0 311.2 jit_solution(13707332915351108414)
XLA Ops:
  0.0 309.5 %denoiser_step.1 = bf16[1,64,2432]{2,1,0:T(8,128)(2,1)} custom-call(bf16[1,64,2432]{2,1,0:T(8,128)(2,1)} %lat.1, bf16[1,64,2432]{2,1,0:T(8,128)(2,1)} %hint.1, bf16[2,3,2432,7296]{3,2,1,0:T(8,128)(2,1)} %in_qkv.1, bf16[2,3,2432,2432]{3,2,1,0:T(8,128)(2,1)} %bitcast.in_proj, bf16[2,3,2432,9728]{3,2,1,0:T(8,128)(2,1)} %in_up.1, ...), custom_call_target="tpu_custom_call" | custom-call | tf_op jit(solution)/shard_map/denoiser_step/pallas_call | solution.py:677
  309.5 1.7 copy.16
